TPU v7x, 128 devices: a whole 4x4x4 slice. The times are simulated.
128 devices in a mesh: dp: 8 (over y, z_lo), fsdp: 16 (over x, z_hi, core).
Axes of the slice: x: 4, y: 4, z: 4 (z_hi: 2, z_lo: 2; z = z_hi * 2 + z_lo), core: 2. Of those that a mesh axis runs over, the one named last changes fastest.
Arguments:
- latent: bfloat16 [128, 1024, 320], P(('dp', 'fsdp')), may hold values from -6 to 6
- hint: bfloat16 [128, 1024, 320], P(('dp', 'fsdp')), may hold values from -48 to 48
- timestep: int32 [128], P(('dp', 'fsdp')), may hold values from 0 to 999
- skip_grad: bfloat16 [128, 1024, 320], P(('dp', 'fsdp')), may hold values from -6 to 6
- frozen_one: bfloat16 [2880, 320], P('fsdp'), may hold values from -0.109375 to 0.109375
- frozen_two: bfloat16 [2880, 320], P('fsdp'), may hold values from -0.109375 to 0.109375
- time_weight: bfloat16 [320, 1280], P('fsdp'), may hold values from -0.3125 to 0.3125
- frozen_emb: bfloat16 [1280, 320], P('fsdp'), may hold values from -0.15625 to 0.15625
- train_one: bfloat16 [2880, 320], P('fsdp'), may hold values from -0.109375 to 0.109375
- train_two: bfloat16 [2880, 320], P('fsdp'), may hold values from -0.109375 to 0.109375
- train_emb: bfloat16 [1280, 320], P('fsdp'), may hold values from -0.15625 to 0.15625
- zero_weight: bfloat16 [320, 320], P('fsdp'), may hold values from -0.3125 to 0.3125
Outputs:
- skip: bfloat16 [128, 1024, 320], P(('dp', 'fsdp'))
- grad_one: float32 [2880, 320], P('fsdp')
- grad_two: float32 [2880, 320], P('fsdp')
- grad_emb: float32 [1280, 320], P('fsdp')
- grad_zero: float32 [320, 320], P('fsdp')
- grad_norm: float32 [], replicated
All inputs are finite; a program needn't handle non-finite values.
Results may differ from a plain program's by a relative error of at most 0.018.
Values may be sent and summed in bfloat16 or wider, within the bound.
A program may use at most 128 MiB of HBM per device.

v0:
```python
import math

import jax
import jax.numpy as jnp
from jax import lax
from jax.experimental import pallas as pl
from jax.experimental.pallas import tpu as pltpu
from jax.sharding import PartitionSpec as P

COLS = 64


clip_limit = 1.0


def sent_together(arrays, axis, dim, along):
    both = jnp.concatenate(arrays, axis=along)
    out, at, gathered = (lax.all_gather(both, axis, axis=dim, tiled=True), 0, [])
    for a in arrays:
        gathered.append(lax.slice_in_dim(out, at, at + a.shape[along], axis=along))
        at += a.shape[along]
    return tuple(gathered)


def laid_out(tiles, dim):
    tiles = jnp.moveaxis(tiles, 0, dim)
    shape = tiles.shape
    return tiles.reshape(*shape[:dim], shape[dim] * shape[dim + 1], *shape[dim + 2 :])


def gather_packed(arrays, axis, dims):
    vector = jnp.concatenate([a.reshape(-1) for a in arrays])
    lines, at, gathered = (lax.all_gather(vector, axis), 0, [])
    for a, dim in zip(arrays, dims):
        tiles = lines[:, at : at + a.size].reshape(-1, *a.shape)
        gathered.append(laid_out(tiles, dim))
        at += a.size
    return tuple(gathered)


def cut_along(value, dim, size):
    before, after = (value.shape[:dim], value.shape[dim + 1 :])
    return jnp.moveaxis(value.reshape(*before, size, -1, *after), dim, 0)


def sum_packed(arrays, axis, dims):
    size = lax.axis_size(axis)
    tiles = [cut_along(a, dim, size) for a, dim in zip(arrays, dims)]
    lines = jnp.concatenate([b.reshape(size, -1) for b in tiles], axis=1)
    span = max(16, -(-lines.shape[1] // 1024) * 8)
    lines = jnp.pad(lines, ((0, 0), (0, span * 128 - lines.shape[1]))).reshape(-1, 128)
    vector, at, gathered = (lax.psum_scatter(lines, axis, tiled=True).reshape(-1), 0, [])
    for b in tiles:
        part = b[0]
        gathered.append(vector[at : at + part.size].reshape(part.shape))
        at += part.size
    return tuple(gathered)


def sent_to_all(value, axis):
    copies = jnp.broadcast_to(value, (lax.axis_size(axis), *value.shape))
    return lax.all_to_all(copies, axis, split_axis=0, concat_axis=0, tiled=True)


def taken_together(value, axis):
    return sent_to_all(value, axis).astype(jnp.float32).sum(axis=0)


def of_everyone(value, axis):
    everything = sent_to_all(value, axis)
    return jnp.sum(everything, axis=0)


POS = 1024
C = 320
TILE = 128
STEPS = POS // TILE
MT = 256
F32 = jnp.float32
BF = jnp.bfloat16
EPS = 1e-05
COUNT = POS * 10.0


def rows(i, size, base=0):
    return pl.ds(pl.multiple_of(i * size + base, 16), size)


def group_matrix():
    r = lax.broadcasted_iota(jnp.int32, (C, C), 0)
    c = lax.broadcasted_iota(jnp.int32, (C, C), 1)
    return ((r * 6554) // 65536 == (c * 6554) // 65536).astype(F32)


def fold(x):
    return x.reshape(TILE // 8, 8, C).sum(axis=0)


def group_mean(part, g_ref):
    total = jnp.dot(part, g_ref[...], preferred_element_type=F32, precision=lax.Precision.HIGHEST)
    return jnp.sum(total, axis=0, keepdims=True) * (1.0 / COUNT)


def stats(read, g_ref):
    zero = jnp.zeros((8, C), F32)
    mean = group_mean(lax.fori_loop(0, STEPS, lambda i, s: s + fold(read(i)), zero), g_ref)

    def square(i, s):
        d = read(i) - mean
        return s + fold(d * d)

    var = group_mean(lax.fori_loop(0, STEPS, square, zero), g_ref)
    return mean, lax.rsqrt(var + EPS)


def put_shifted(x, ref, i, order):
    j = lax.broadcasted_iota(jnp.int32, (TILE, C), 0) % COLS
    before = jnp.where(j == 0, 0.0, pltpu.roll(x, 1, 0)).astype(BF)
    after = jnp.where(j == COLS - 1, 0.0, pltpu.roll(x, TILE - 1, 0)).astype(BF)
    mid = x.astype(BF)
    parts = (before, mid, after) if order > 0 else (after, mid, before)
    ref[rows(i, TILE, COLS), :] = jnp.concatenate(parts, axis=1)


def clear_edges(ref):
    z = jnp.zeros((COLS, ref.shape[1]), ref.dtype)
    ref[0:COLS, :] = z
    ref[COLS + POS : 2 * COLS + POS, :] = z


def normed_silu(read, x3, g_ref):
    mean, inverse = stats(read, g_ref)

    def body(i, c):
        y = (read(i) - mean) * inverse
        put_shifted(y * jax.nn.sigmoid(y), x3, i, 1)
        return c

    lax.fori_loop(0, STEPS, body, 0)


def conv(x3, w_ref, write):
    def body(m, c):
        acc = None
        for a in range(3):
            t = jnp.dot(
                x3[rows(m, MT, a * COLS), :], w_ref[a * 960 : (a + 1) * 960, :], preferred_element_type=F32
            )
            acc = t if acc is None else acc + t
        write(m, acc)
        return c

    lax.fori_loop(0, POS // MT, body, 0)


def conv_back(d3, w_ref, write):
    def body(m, c):
        acc = None
        for a in range(3):
            for b in range(3):
                k = 3 * a + b
                t = lax.dot_general(
                    d3[rows(m, MT, (2 - a) * COLS), b * C : (b + 1) * C],
                    w_ref[k * C : (k + 1) * C, :],
                    (((1,), (1,)), ((), ())),
                    preferred_element_type=F32,
                )
                acc = t if acc is None else acc + t
        write(m, acc)
        return c

    lax.fori_loop(0, POS // MT, body, 0)


def conv_grads(x3, dp, out):
    for b in range(3):
        lhs = x3[COLS : COLS + POS, b * C : (b + 1) * C]
        for a in range(3):
            k = 3 * a + b
            t = lax.dot_general(
                lhs, dp[128 - 64 * a : 128 - 64 * a + POS, :], (((0,), (0,)), ((), ())), preferred_element_type=F32
            )
            out[k * C : (k + 1) * C, :] = t.astype(BF)


def kernel(
    lat, hint, sg, ef, et, f1, f2, t1, t2, zw,
    skip, dw1, dw2, dz, esum,
    g_ref, xa, xb, d3, dp, y1, p, ctl,
):
    g_ref[...] = group_matrix()
    for r in (xa, xb, d3, dp):
        clear_edges(r)

    def latent_at(i):
        return lat[rows(i, TILE), :].astype(F32)

    def mixed_at(i):
        return latent_at(i) + hint[rows(i, TILE), :].astype(F32)

    def p_at(i):
        return p[rows(i, TILE), :]

    normed_silu(mixed_at, xa, g_ref)

    def dc_body(i, c):
        d = lax.dot_general(sg[rows(i, TILE), :], zw[...], (((1,), (1,)), ((), ())), preferred_element_type=F32)
        d = d.astype(BF).astype(F32)
        dp[rows(i, TILE, COLS), :] = d.astype(BF)
        put_shifted(d, d3, i, -1)
        return c

    lax.fori_loop(0, STEPS, dc_body, 0)

    def put_p(e):
        def write(m, acc):
            p[rows(m, MT), :] = acc + e
        return write

    conv(xa, t1, put_p(et[...]))
    mean, inverse = stats(p_at, g_ref)

    def y_body(i, c):
        y = (p_at(i) - mean) * inverse
        y1[rows(i, TILE), :] = y
        put_shifted(y * jax.nn.sigmoid(y), xb, i, 1)
        return c

    lax.fori_loop(0, STEPS, y_body, 0)
    conv_grads(xb, dp, dw2)

    def write_da(m, acc):
        p[rows(m, MT), :] = acc

    conv_back(d3, t2, write_da)
    zero = jnp.zeros((8, C), F32)

    def dy_body(i, s):
        y = y1[rows(i, TILE), :]
        sig = jax.nn.sigmoid(y)
        dy = p_at(i) * sig * (1.0 + y * (1.0 - sig))
        p[rows(i, TILE), :] = dy
        return s[0] + fold(dy), s[1] + fold(dy * y)

    s1, s2 = lax.fori_loop(0, STEPS, dy_body, (zero, zero))
    m1, m2 = group_mean(s1, g_ref), group_mean(s2, g_ref)

    def dp_body(i, s):
        d = (p_at(i) - m1 - y1[rows(i, TILE), :] * m2) * inverse
        dp[rows(i, TILE, COLS), :] = d.astype(BF)
        return s + fold(d)

    esum[...] = jnp.sum(lax.fori_loop(0, STEPS, dp_body, zero), axis=0, keepdims=True)
    conv_grads(xa, dp, dw1)

    def write_control(m, acc):
        mixed = lat[rows(m, MT), :].astype(F32) + hint[rows(m, MT), :].astype(F32)
        ctl[rows(m, MT), :] = (mixed + acc).astype(BF)

    conv(xb, t2, write_control)
    dz[...] = lax.dot_general(ctl[...], sg[...], (((0,), (0,)), ((), ())), preferred_element_type=F32).astype(BF)

    normed_silu(latent_at, xa, g_ref)
    conv(xa, f1, put_p(ef[...]))
    normed_silu(p_at, xb, g_ref)

    def write_skip(m, acc):
        out = lat[rows(m, MT), :].astype(F32) + acc
        out = out + jnp.dot(ctl[rows(m, MT), :], zw[...], preferred_element_type=F32)
        skip[rows(m, MT), :] = out.astype(BF)

    conv(xb, f2, write_skip)


SCRATCH = [
    pltpu.VMEM((C, C), F32),
    pltpu.VMEM((POS + 2 * COLS, 3 * C), BF),
    pltpu.VMEM((POS + 2 * COLS, 3 * C), BF),
    pltpu.VMEM((POS + 2 * COLS, 3 * C), BF),
    pltpu.VMEM((POS + 2 * COLS, C), BF),
    pltpu.VMEM((POS, C), F32),
    pltpu.VMEM((POS, C), F32),
    pltpu.VMEM((POS, C), BF),
]


def compute(lat, hint, sg, ef, et, f1, f2, t1, t2, zw):
    vm = pl.BlockSpec(memory_space=pltpu.VMEM)
    return pl.pallas_call(
        kernel,
        out_shape=(
            jax.ShapeDtypeStruct((POS, C), BF),
            jax.ShapeDtypeStruct((9 * C, C), BF),
            jax.ShapeDtypeStruct((9 * C, C), BF),
            jax.ShapeDtypeStruct((C, C), BF),
            jax.ShapeDtypeStruct((1, C), F32),
        ),
        in_specs=[vm] * 10,
        out_specs=[vm] * 5,
        scratch_shapes=SCRATCH,
        compiler_params=pltpu.CompilerParams(vmem_limit_bytes=64000000),
    )(lat, hint, sg, ef, et, f1, f2, t1, t2, zw)


def time_embed(timestep, time_weight):
    half = time_weight.shape[0] // 2
    freqs = jnp.exp(-math.log(10000.0) * jnp.arange(half).astype(jnp.float32) / half)
    angles = timestep.astype(jnp.float32)[:, None] * freqs[None, :]
    wave = jnp.concatenate([jnp.cos(angles), jnp.sin(angles)], axis=1).astype(jnp.bfloat16)
    return jax.nn.silu(jnp.dot(wave, time_weight, preferred_element_type=jnp.float32)).astype(
        jnp.bfloat16
    )


def shards(
    latent,
    hint,
    timestep,
    skip_grad,
    frozen_one,
    frozen_two,
    time_weight,
    frozen_emb,
    train_one,
    train_two,
    train_emb,
    zero_weight,
):
    frozen_full = (
        *sent_together((frozen_one, frozen_two), "fsdp", 0, 1),
        lax.all_gather(time_weight, "fsdp", axis=0, tiled=True),
        lax.all_gather(frozen_emb, "fsdp", axis=0, tiled=True),
    )
    train_full = gather_packed((train_one, train_two, train_emb, zero_weight), "fsdp", (0, 0, 0, 0))
    emb = time_embed(timestep, frozen_full[2])
    frozen_row = jnp.dot(emb, frozen_full[3], preferred_element_type=F32)
    train_row = jnp.dot(emb, train_full[2], preferred_element_type=F32)
    skip, dw1, dw2, dz, esum = compute(
        latent[0], hint[0], skip_grad[0], frozen_row, train_row,
        frozen_full[0], frozen_full[1], train_full[0], train_full[1], train_full[3],
    )
    skips = skip[None]
    grads = (dw1, dw2, emb[0].astype(F32)[:, None] * esum, dz)
    partial_rows = tuple(
        (
            part.astype(jnp.float32)
            for part in sum_packed(
                (
                    grads[0].astype(jnp.bfloat16),
                    grads[1].astype(jnp.bfloat16),
                    grads[2].astype(jnp.bfloat16),
                    grads[3].astype(jnp.bfloat16),
                ),
                "fsdp",
                (0, 0, 0, 0),
            )
        )
    )
    owned = (
        taken_together(partial_rows[0].astype(jnp.bfloat16), "dp").astype(jnp.float32),
        taken_together(partial_rows[1].astype(jnp.bfloat16), "dp").astype(jnp.float32),
        taken_together(partial_rows[2].astype(jnp.bfloat16), "dp").astype(jnp.float32),
        taken_together(partial_rows[3].astype(jnp.bfloat16), "dp").astype(jnp.float32),
    )
    local_sum = sum((jnp.sum(item * item) for item in owned))
    total = of_everyone(local_sum, "fsdp")
    grad_norm = jnp.sqrt(total + 1e-06)
    scale = jnp.minimum(1.0, clip_limit / grad_norm)
    return (
        skips,
        owned[0] * scale,
        owned[1] * scale,
        owned[2] * scale,
        owned[3] * scale,
        grad_norm,
    )


def solution(mesh):
    in_specs = (
        P(("dp", "fsdp"), None, None),
        P(("dp", "fsdp"), None, None),
        P(("dp", "fsdp")),
        P(("dp", "fsdp"), None, None),
        P("fsdp", None),
        P("fsdp", None),
        P("fsdp", None),
        P("fsdp", None),
        P("fsdp", None),
        P("fsdp", None),
        P("fsdp", None),
        P("fsdp", None),
    )
    out_specs = (
        P(("dp", "fsdp"), None, None),
        P("fsdp", None),
        P("fsdp", None),
        P("fsdp", None),
        P("fsdp", None),
        P(),
    )
    return jax.shard_map(shards, mesh=mesh, in_specs=in_specs, out_specs=out_specs, check_vma=False)
```

profile of v0, /device:TPU:1, one launch (start us, length us, event | category | flops | bytes accessed | tf_op | source)
XLA Modules:
  0.0 435.0 jit_solution(6514596122293501890)
XLA Ops:
  7.2 1.8 maximum_bitcast_fusion
  13.1 4.1 reshape.103
  18.1 30.6 %all-gather.1 = bf16[16,20,1280]{2,1,0:T(8,128)(2,1)S(1)} all-gather(bf16[1,20,1280]{2,1,0:T(8,128)(2,1)S(1)} %bitcast.24), channel_id=1, replica_groups=mesh['dp'=8,'fsdp'=16] {'fsdp'}, dimensions={0}, use_global_device_ids=true | all-gather | bytes 870400 | tf_op jit(solution)/shard_map/all_gather | solution.py:331
  53.0 1.9 mul.93
  54.9 26.1 %all_gather.16 = bf16[1280,320]{1,0:T(8,128)(2,1)S(1)} all-gather(bf16[80,320]{1,0:T(8,128)(2,1)S(1)} %copy-done.8), channel_id=1, replica_groups=mesh['dp'=8,'fsdp'=16] {'fsdp'}, dimensions={0}, use_global_device_ids=true | all-gather | bytes 870400 | tf_op jit(solution)/shard_map/all_gather | solution.py:332
  81.8 4.7 %reshape.106 = bf16[2880,640]{1,0:T(8,128)(2,1)} reshape(bf16[16,180,640]{2,1,0:T(8,128)(2,1)} %all-gather.9.cloned.1.call-done) | data formatting | bytes 7372800
  86.4 5.7 %fusion.8 = (bf16[2880,320]{1,0:T(8,128)(2,1)}, bf16[2880,320]{1,0:T(8,128)(2,1)}) fusion(bf16[2880,640]{1,0:T(8,128)(2,1)} %reshape.106), kind=kLoop, calls=%fused_computation.31 | loop fusion | bytes 7372800 | tf_op jit(solution)/shard_map/slice | solution.py:20
  92.2 64.5 %all-gather.7.cloned.1.call-done = bf16[16,1,147200]{2,1,0:T(2,128)(2,1)} async-done(((bf16[1,1,147200]{2,1,0:T(2,128)(2,1)}), bf16[16,1,147200]{2,1,0:T(2,128)(2,1)}) %all-gather.7.cloned.1.call-update) | async-done | bytes 4710416 | tf_op jit(solution)/shard_map/all_gather | solution.py:33
  156.7 5.0 %copy.60 = bf16[16,1,147200]{2,0,1:T(8,128)(2,1)S(1)} copy(bf16[16,1,147200]{2,1,0:T(2,128)(2,1)} %all-gather.7.cloned.1.call-done) | data formatting | bytes 9420800
  162.6 1.5 fusion.7
  164.2 1.9 reshape_reshape.22
  166.9 5.0 %reshape_reshape.23.t1 = bf16[2880,320]{1,0:T(8,128)(2,1)} reshape(bf16[16,57600]{1,0:T(8,128)(2,1)} %get-tuple-element.59) | data formatting | bytes 3686400 | tf_op jit(solution)/shard_map/reshape;reshape | solution.py:28
  172.0 3.8 reshape_reshape.24.t2
  176.8 48.5 %shard_map.163 = (bf16[1024,320]{1,0:T(8,128)(2,1)}, bf16[2880,320]{1,0:T(8,128)(2,1)}, bf16[2880,320]{1,0:T(8,128)(2,1)}, bf16[320,320]{1,0:T(8,128)(2,1)}, f32[1,320]{1,0:T(1,128)}) custom-call(bf16[1024,320]{1,0:T(8,128)(2,1)} %bitcast.20, bf16[1024,320]{1,0:T(8,128)(2,1)} %bitcast.21, bf16[1024,320]{1,0:T(8,128)(2,1)} %bitcast.22, f32[1,320]{1,0:T(1,128)} %fusion.10.ef, ...), custom_call_target="tpu_custom_call" | custom-call | tf_op jit(solution)/shard_map/pallas_call | solution.py:289
  226.7 4.3 reshape_reshape.26
  231.1 5.0 %reshape_reshape.27 = bf16[16,57600]{1,0:T(8,128)(2,1)} reshape(bf16[2880,320]{1,0:T(8,128)(2,1)} %get-tuple-element.13) | data formatting | bytes 3686400 | tf_op jit(solution)/shard_map/reshape;reshape | solution.py:49
  236.1 1.9 reshape_reshape.28
  238.0 1.2 multiply_convert_fusion
  239.5 19.5 %fusion.6 = bf16[16,147456]{1,0:T(8,128)(2,1)} fusion(bf16[16,6400]{1,0:T(8,128)(2,1)S(1)} %copy-done.2, bf16[16,25600]{1,0:T(8,128)(2,1)S(1)} %multiply_convert_fusion, bf16[16,57600]{1,0:T(8,128)(2,1)S(1)} %copy-done, bf16[16,57600]{1,0:T(8,128)(2,1)S(1)} %reshape_reshape.26), kind=kLoop, calls=%fused_computation.7 | loop fusion | flops 30670848 | bytes 9428992 | tf_op jit(solution)/shard_map/concatenate | solution.py:49
  259.0 5.3 %reshape.94 = bf16[18432,128]{1,0:T(8,128)(2,1)} reshape(bf16[16,147456]{1,0:T(8,128)(2,1)} %fusion.6) | data formatting | bytes 9437184 | tf_op jit(solution)/shard_map/reshape | solution.py:51
  264.3 78.7 %reduce-scatter.2.cloned.1.call-done = bf16[1152,128]{1,0:T(8,128)(2,1)} async-done(((bf16[18432,128]{1,0:T(8,128)(2,1)}), bf16[1152,128]{1,0:T(8,128)(2,1)}) %reduce-scatter.2.cloned.1.call-update) | async-done | bytes 294928 | tf_op jit(solution)/shard_map/reduce_scatter | solution.py:52
  344.6 4.1 all-to-all-start.3
  349.6 4.4 %all-to-all-done.3 = bf16[8,20,320]{2,1,0:T(8,128)(2,1)S(1)} async-done(((bf16[8,20,320]{2,1,0:T(8,128)(2,1)}), bf16[8,20,320]{2,1,0:T(8,128)(2,1)S(1)}, u32[]{:S(2)}, u32[]{:S(2)}) %all-to-all-start.3) | async-done | bytes 102432 | tf_op jit(solution)/shard_map/all_to_all | solution.py:62
  354.8 3.5 all-to-all-start.2
  358.5 6.5 %all-to-all-done.2 = bf16[8,80,320]{2,1,0:T(8,128)(2,1)S(1)} async-done(((bf16[8,80,320]{2,1,0:T(8,128)(2,1)}), bf16[8,80,320]{2,1,0:T(8,128)(2,1)S(1)}, u32[]{:S(2)}, u32[]{:S(2)}) %all-to-all-start.2) | async-done | bytes 409632 | tf_op jit(solution)/shard_map/all_to_all | solution.py:62
  366.1 3.7 all-to-all-start.1
  370.0 12.3 %all-to-all-done.1 = bf16[8,180,320]{2,1,0:T(8,128)(2,1)S(1)} async-done(((bf16[8,180,320]{2,1,0:T(8,128)(2,1)}), bf16[8,180,320]{2,1,0:T(8,128)(2,1)S(1)}, u32[]{:S(2)}, u32[]{:S(2)}) %all-to-all-start.1) | async-done | bytes 921632 | tf_op jit(solution)/shard_map/all_to_all | solution.py:62
  383.4 5.8 %all-to-all-start = ((bf16[8,180,320]{2,1,0:T(8,128)(2,1)}), bf16[8,180,320]{2,1,0:T(8,128)(2,1)S(1)}, u32[]{:S(2)}, u32[]{:S(2)}) async-start(bf16[8,180,320]{2,1,0:T(8,128)(2,1)} %broadcast_in_dim.22), calls=%async_computation.1 | async-start | bytes 2260992 | tf_op jit(solution)/shard_map/all_to_all | solution.py:62
  391.9 11.7 %all-to-all-done = bf16[8,180,320]{2,1,0:T(8,128)(2,1)S(1)} async-done(((bf16[8,180,320]{2,1,0:T(8,128)(2,1)}), bf16[8,180,320]{2,1,0:T(8,128)(2,1)S(1)}, u32[]{:S(2)}, u32[]{:S(2)}) %all-to-all-start) | async-done | bytes 921632 | tf_op jit(solution)/shard_map/all_to_all | solution.py:62
  408.3 7.8 %all-to-all-start.4 = ((f32[16,1,1]{2,1,0:T(1,128)}), f32[16,1,1]{2,1,0:T(1,128)S(1)}, u32[]{:S(2)}, u32[]{:S(2)}) async-start(f32[16,1,1]{2,1,0:T(1,128)} %broadcast_in_dim.26), calls=%async_computation.5 | async-start | bytes 16384 | tf_op jit(solution)/shard_map/all_to_all | solution.py:62
  416.1 2.2 copy.53
  418.3 4.7 %all-to-all-done.4 = f32[16,1,1]{2,1,0:T(1,128)S(1)} async-done(((f32[16,1,1]{2,1,0:T(1,128)}), f32[16,1,1]{2,1,0:T(1,128)S(1)}, u32[]{:S(2)}, u32[]{:S(2)}) %all-to-all-start.4) | async-done | bytes 96 | tf_op jit(solution)/shard_map/all_to_all | solution.py:62
  (75 shorter events, 28.0 us)
Async XLA Ops:
  7.2 11.0 %copy-start.7 = (bf16[20,1280]{1,0:T(8,128)(2,1)S(1)}, bf16[20,1280]{1,0:T(8,128)(2,1)}, u32[]{:S(2)}) copy-start(bf16[20,1280]{1,0:T(8,128)(2,1)} %param.18) | copy-start | bytes 153604
  7.2 74.6 %all-gather.9.cloned.1.call-start = ((), (), s32[]{:S(2)}) async-start(), calls=%async_computation.8 | async-start | bytes 4003840 | tf_op jit(solution)/shard_map/all_gather | solution.py:18
  9.0 147.6 %all-gather.7.cloned.1.call-start = ((), (), s32[]{:S(2)}) async-start(), calls=%async_computation.7 | async-start | bytes 10009600 | tf_op jit(solution)/shard_map/all_gather | solution.py:33
  17.2 32.0 %copy-start.3 = (bf16[1,1024,320]{1,2,0:T(8,128)(2,1)S(1)}, bf16[1,1024,320]{1,2,0:T(8,128)(2,1)}, u32[]{:S(2)}) copy-start(bf16[1,1024,320]{1,2,0:T(8,128)(2,1)} %param.12) | copy-start | bytes 1966084
  17.2 325.8 %reduce-scatter.2.cloned.1.call-start = ((), (), s32[]{:S(2)}) async-start(), calls=%async_computation.6 | async-start | bytes 5013504 | tf_op jit(solution)/shard_map/reduce_scatter | solution.py:52
  48.7 1.7 copy-start.4
  48.9 2.7 copy-start.5
  53.0 1.9 copy-start.8
  231.1 6.9 %copy-start.1 = (f32[16,25600]{1,0:T(8,128)S(1)}, f32[16,25600]{1,0:T(8,128)}, u32[]{:S(2)}) copy-start(f32[16,25600]{1,0:T(8,128)} %mul.93) | copy-start | bytes 4915204
  238.0 1.6 copy-start
  238.0 1.6 copy-start.2
  343.0 15.3 %copy-start.6 = (bf16[1152,128]{1,0:T(8,128)(2,1)S(1)}, bf16[1152,128]{1,0:T(8,128)(2,1)}, u32[]{:S(2)}) copy-start(bf16[1152,128]{1,0:T(8,128)(2,1)} %reduce-scatter.2.cloned.1.call-done) | copy-start | bytes 884740
  344.6 9.4 %all-to-all-start.3 = ((bf16[8,20,320]{2,1,0:T(8,128)(2,1)}), bf16[8,20,320]{2,1,0:T(8,128)(2,1)S(1)}, u32[]{:S(2)}, u32[]{:S(2)}) async-start(bf16[8,20,320]{2,1,0:T(8,128)(2,1)} %broadcast_in_dim.25), calls=%async_computation.4 | async-start | bytes 294912 | tf_op jit(solution)/shard_map/all_to_all | solution.py:62
  354.8 10.2 %all-to-all-start.2 = ((bf16[8,80,320]{2,1,0:T(8,128)(2,1)}), bf16[8,80,320]{2,1,0:T(8,128)(2,1)S(1)}, u32[]{:S(2)}, u32[]{:S(2)}) async-start(bf16[8,80,320]{2,1,0:T(8,128)(2,1)} %broadcast_in_dim.24), calls=%async_computation.3 | async-start | bytes 983040 | tf_op jit(solution)/shard_map/all_to_all | solution.py:62
  366.1 16.1 %all-to-all-start.1 = ((bf16[8,180,320]{2,1,0:T(8,128)(2,1)}), bf16[8,180,320]{2,1,0:T(8,128)(2,1)S(1)}, u32[]{:S(2)}, u32[]{:S(2)}) async-start(bf16[8,180,320]{2,1,0:T(8,128)(2,1)} %broadcast_in_dim.23), calls=%async_computation.2 | async-start | bytes 2260992 | tf_op jit(solution)/shard_map/all_to_all | solution.py:62
  383.4 20.3 %all-to-all-start = ((bf16[8,180,320]{2,1,0:T(8,128)(2,1)}), bf16[8,180,320]{2,1,0:T(8,128)(2,1)S(1)}, u32[]{:S(2)}, u32[]{:S(2)}) async-start(bf16[8,180,320]{2,1,0:T(8,128)(2,1)} %broadcast_in_dim.22), calls=%async_computation.1 | async-start | bytes 2260992 | tf_op jit(solution)/shard_map/all_to_all | solution.py:62
  408.3 14.8 %all-to-all-start.4 = ((f32[16,1,1]{2,1,0:T(1,128)}), f32[16,1,1]{2,1,0:T(1,128)S(1)}, u32[]{:S(2)}, u32[]{:S(2)}) async-start(f32[16,1,1]{2,1,0:T(1,128)} %broadcast_in_dim.26), calls=%async_computation.5 | async-start | bytes 16384 | tf_op jit(solution)/shard_map/all_to_all | solution.py:62
Sparse Core Ops, SparseCore 0:
  11.0 67.4 all-gather.8
  81.4 75.1 all-gather.6
  264.4 78.5 reduce-scatter.1
where the time goes:
time: 440 us; the launch traced here: 435 us
  waiting for transfers between devices  183 us (42%)
  local copies, waits for them, and re-layouts  69.9 us (16%)
  blocking collectives  56.7 us (13%)
  Pallas kernels  48.5 us (11%)
  other arithmetic  30.9 us (7%)
  starting transfers between devices  25 us (6%)
  between operations  19.3 us (4%)
    reduce_scatter x1, waiting for transfers between devices, sum_packed(): lax.psum_scatter(lines, axis, tiled=True).reshape(-1)  78.7 us
    all_gather x1, waiting for transfers between devices, gather_packed(): lines, at, gathered = (lax.all_gather(vector, axis), 0, [])  64.5 us
    pallas_call x1, Pallas kernels, compute(): pl.pallas_call(kernel, out_shape=(jax.ShapeDtypeStruct((POS, C), BF), jax...  48.5 us
    all_to_all x5, waiting for transfers between devices, sent_to_all(): return lax.all_to_all(copies, axis, split_axis=0, concat_axis=0, tiled=True)  39.6 us
    all_gather x1, blocking collectives, shards(): lax.all_gather(time_weight, 'fsdp', axis=0, tiled=True)  30.6 us
    all_gather x1, blocking collectives, shards(): lax.all_gather(frozen_emb, 'fsdp', axis=0, tiled=True)  26.1 us
    all_to_all x5, starting transfers between devices, sent_to_all(): return lax.all_to_all(copies, axis, split_axis=0, concat_axis=0, tiled=True)  24.9 us
    unnamed x26, local copies, waits for them, and re-layouts  20 us
  transfers between devices with their start and end apart: 8, of which 7 were waited for; matrix products, arithmetic and copies ran while one was open for 7% of the time, Pallas kernels for 0%

commit v1 on v0

v1 whole, which is shorter than its diff:
```python
import math

import jax
import jax.numpy as jnp
from jax import lax
from jax.experimental import pallas as pl
from jax.experimental.pallas import tpu as pltpu
from jax.sharding import PartitionSpec as P

COLS = 64
POS = 1024
C = 320
TEMB = 1280
TILE = 128
STEPS = POS // TILE
MT = 256
HALF = 90
HALF_Z = 100
CUT = 48
F32 = jnp.float32
BF = jnp.bfloat16
EPS = 1e-05
COUNT = POS * 10.0
clip_limit = 1.0
EXACT = lax.Precision.HIGHEST
MESH = pl.DeviceIdType.MESH


def rows(i, size, base=0):
    return pl.ds(pl.multiple_of(i * size + base, 16), size)


def group_matrix():
    r = lax.broadcasted_iota(jnp.int32, (C, C), 0)
    c = lax.broadcasted_iota(jnp.int32, (C, C), 1)
    return ((r * 6554) // 65536 == (c * 6554) // 65536).astype(F32)


def fold(x):
    return x.reshape(TILE // 8, 8, C).sum(axis=0)


def group_mean(part, g_ref):
    total = jnp.dot(part, g_ref[...], preferred_element_type=F32, precision=lax.Precision.HIGHEST)
    return jnp.sum(total, axis=0, keepdims=True) * (1.0 / COUNT)


def stats(read, g_ref):
    zero = jnp.zeros((8, C), F32)
    mean = group_mean(lax.fori_loop(0, STEPS, lambda i, s: s + fold(read(i)), zero), g_ref)

    def square(i, s):
        d = read(i) - mean
        return s + fold(d * d)

    var = group_mean(lax.fori_loop(0, STEPS, square, zero), g_ref)
    return mean, lax.rsqrt(var + EPS)


def put_shifted(x, ref, i, order):
    j = lax.broadcasted_iota(jnp.int32, (TILE, C), 0) % COLS
    before = jnp.where(j == 0, 0.0, pltpu.roll(x, 1, 0)).astype(BF)
    after = jnp.where(j == COLS - 1, 0.0, pltpu.roll(x, TILE - 1, 0)).astype(BF)
    mid = x.astype(BF)
    parts = (before, mid, after) if order > 0 else (after, mid, before)
    ref[rows(i, TILE, COLS), :] = jnp.concatenate(parts, axis=1)


def clear_edges(ref):
    z = jnp.zeros((COLS, ref.shape[1]), ref.dtype)
    ref[0:COLS, :] = z
    ref[COLS + POS : 2 * COLS + POS, :] = z


def normed_silu(read, x3, g_ref):
    mean, inverse = stats(read, g_ref)

    def body(i, c):
        y = (read(i) - mean) * inverse
        put_shifted(y * jax.nn.sigmoid(y), x3, i, 1)
        return c

    lax.fori_loop(0, STEPS, body, 0)


def conv(x3, w_ref, write):
    def body(m, c):
        acc = None
        for a in range(3):
            t = jnp.dot(
                x3[rows(m, MT, a * COLS), :], w_ref[a * 960 : (a + 1) * 960, :], preferred_element_type=F32
            )
            acc = t if acc is None else acc + t
        write(m, acc)
        return c

    lax.fori_loop(0, POS // MT, body, 0)


def conv_back(d3, w_ref, write):
    def body(m, c):
        acc = None
        for a in range(3):
            for b in range(3):
                k = 3 * a + b
                t = lax.dot_general(
                    d3[rows(m, MT, (2 - a) * COLS), b * C : (b + 1) * C],
                    w_ref[k * C : (k + 1) * C, :],
                    (((1,), (1,)), ((), ())),
                    preferred_element_type=F32,
                )
                acc = t if acc is None else acc + t
        write(m, acc)
        return c

    lax.fori_loop(0, POS // MT, body, 0)


def turned(src, dst):
    def body(i, c):
        cols = pl.ds(pl.multiple_of(i * TILE, TILE), TILE)
        dst[rows(i, TILE), :] = src[:, cols].astype(F32).T.astype(BF)
        return c

    lax.fori_loop(0, STEPS, body, 0)


def paired(ref, dst, at, size):
    dst[at : at + size, 0:C] = ref[0:size, :]
    dst[at : at + size, C : 2 * C] = ref[size : 2 * size, :]


def add_into(dst, *others):
    total = dst[...].astype(F32)
    for o in others:
        total = total + o[...].astype(F32)
    dst[...] = total.astype(BF)


def kernel(
    lat_t, hint_t, sg_t, wave, f1, f2, tw, fe, t1, t2, te, zw,
    skip, o1, o2, oe, oz, onorm,
    lat, hint, sg, g_ref, xa, xb, xf, d3, dp, y1, p, ctl, dw,
    w1, w2, v1, v2, wz,
    ga, gb, gc, gd,
    wv, pb, pr, rb, rr, em, es, nr,
    out_a, out_b, in_a, in_b, xp_a, xp_b, xq_a, xq_b, zb_a, zb_b, cur_a, cur_b, got_a, got_b,
    g_send, g_recv, e_send, e_recv, r_send, r_recv,
):
    me_dp, me = lax.axis_index("dp"), lax.axis_index("fsdp")
    core, zh, x = lax.rem(me, 2), lax.rem(me // 2, 2), me // 4
    y, zl = me_dp // 2, lax.rem(me_dp, 2)
    oc, oh, ol = 1 - core, 1 - zh, 1 - zl
    xr, xl, xo = lax.rem(x + 1, 4), lax.rem(x + 3, 4), lax.rem(x + 2, 4)
    y_near = y + 1 - 2 * lax.rem(y, 2)
    right = (me_dp, xr * 4 + zh * 2 + core)
    left = (me_dp, xl * 4 + zh * 2 + core)
    mate = (me_dp, x * 4 + zh * 2 + oc)
    z_b = (y * 2 + ol, x * 4 + oh * 2 + core)
    z_a = (y * 2 + ol, me)
    y_a = (y_near * 2 + zl, me)
    y_b = ((3 - y) * 2 + zl, me)

    started = []

    def send(src, dst, ssem, rsem, to):
        c = pltpu.make_async_remote_copy(
            src_ref=src, dst_ref=dst, send_sem=ssem, recv_sem=rsem, device_id=to, device_id_type=MESH
        )
        c.start()
        started.append(c)

    def landed(ref, rsem):
        pltpu.make_async_remote_copy(
            src_ref=ref, dst_ref=ref, send_sem=rsem, recv_sem=rsem, device_id=mate, device_id_type=MESH
        ).wait_recv()

    gathered = (ga, gb, gc, gd)
    own = x * 2 + zh
    paired(t1, ga.at[core, own], 0, HALF)
    paired(zw, ga.at[core, own], HALF, 10)
    barrier = pltpu.get_barrier_semaphore()

    def greet(k, c):
        pl.semaphore_signal(barrier, inc=1, device_id=(me_dp, lax.rem(me + k, 16)), device_id_type=MESH)
        return c

    lax.fori_loop(1, 16, greet, 0)
    for to in (z_b, z_a, y_a, y_b):
        pl.semaphore_signal(barrier, inc=1, device_id=to, device_id_type=MESH)
    paired(t2, gb.at[core, own], 0, HALF)
    paired(f1, gc.at[core, own], 0, HALF)
    paired(f2, gd.at[core, own], 0, HALF)
    wv[me] = wave[...]
    pl.semaphore_wait(barrier, 19)

    def block(w, j):
        return gathered[w].at[core, j]

    def pass_on(w, j, n):
        send(block(w, j), block(w, j), g_send.at[w, n], g_recv.at[w, 8 + n], mate)

    def low(w, j):
        return gathered[w].at[core, j, pl.ds(0, CUT)]

    def high(w, j):
        return gathered[w].at[core, j, pl.ds(CUT, gathered[w].shape[2] - CUT)]

    def g1(w):
        b = block(w, own)
        send(b, b, g_send.at[w, 8], g_recv.at[w, 0], right)
        send(b, b, g_send.at[w, 9], g_recv.at[w, 1], left)
        send(b, b, g_send.at[w, 10], g_recv.at[w, 2], z_b)
        pass_on(w, own, 0)

    def g2(w):
        jl, jr, jz = xl * 2 + zh, xr * 2 + zh, x * 2 + oh
        landed(block(w, jl), g_recv.at[w, 0])
        send(low(w, jl), low(w, jl), g_send.at[w, 11], g_recv.at[w, 3], right)
        landed(block(w, jr), g_recv.at[w, 1])
        send(high(w, jr), high(w, jr), g_send.at[w, 12], g_recv.at[w, 4], left)
        landed(block(w, jz), g_recv.at[w, 2])
        send(block(w, jz), block(w, jz), g_send.at[w, 13], g_recv.at[w, 5], right)
        send(block(w, jz), block(w, jz), g_send.at[w, 14], g_recv.at[w, 6], left)
        pass_on(w, jl, 1)
        pass_on(w, jr, 2)
        pass_on(w, jz, 3)

    def g3(w):
        jo, jl, jr = xo * 2 + zh, xl * 2 + oh, xr * 2 + oh
        landed(low(w, jo), g_recv.at[w, 3])
        landed(high(w, jo), g_recv.at[w, 4])
        send(block(w, jo), block(w, jo), g_send.at[w, 15], g_recv.at[w, 7], z_b)
        pass_on(w, jo, 4)
        landed(block(w, jl), g_recv.at[w, 5])
        pass_on(w, jl, 5)
        landed(block(w, jr), g_recv.at[w, 6])
        pass_on(w, jr, 6)

    def g4(w):
        jz = xo * 2 + oh
        landed(block(w, jz), g_recv.at[w, 7])
        pass_on(w, jz, 7)

    def g5(w, full):
        order = (
            x * 2 + zh, xl * 2 + zh, xr * 2 + zh, x * 2 + oh, xo * 2 + zh, xl * 2 + oh, xr * 2 + oh, xo * 2 + oh
        )
        for n, j in enumerate(order):
            landed(gathered[w].at[oc, j], g_recv.at[w, 8 + n])
        g = gathered[w]
        for d in range(16):
            for h in range(2):
                full[d * 180 + h * HALF : d * 180 + (h + 1) * HALF, :] = g[
                    d % 2, d // 2, 0:HALF, h * C : (h + 1) * C
                ]

    def spread(n, src_of, dst):
        def body(k, c):
            to = lax.rem(me + k, 16)
            pltpu.make_async_remote_copy(
                src_ref=src_of(to), dst_ref=dst.at[me], send_sem=e_send.at[n, to], recv_sem=e_recv.at[n, me],
                device_id=(me_dp, to), device_id_type=MESH,
            ).start()
            return c

        lax.fori_loop(1, 16, body, 0)

    def spread_wait(n, dst):
        def body(k, c):
            slot = lax.rem(me + k, 16)
            pltpu.make_async_remote_copy(
                src_ref=dst.at[slot], dst_ref=dst.at[slot], send_sem=e_send.at[n, slot], recv_sem=e_recv.at[n, slot],
                device_id=(me_dp, slot), device_id_type=MESH,
            ).wait_recv()
            return c

        lax.fori_loop(1, 16, body, 0)

    def spread_sent(n, src_of, dst):
        def body(k, c):
            to = lax.rem(me + k, 16)
            pltpu.make_async_remote_copy(
                src_ref=src_of(to), dst_ref=dst.at[me], send_sem=e_send.at[n, to], recv_sem=e_recv.at[n, me],
                device_id=(me_dp, to), device_id_type=MESH,
            ).wait_send()
            return c

        lax.fori_loop(1, 16, body, 0)

    def stacked(ref):
        return jnp.concatenate([ref[s] for s in range(16)], axis=0)

    g1(0)
    spread(0, lambda to: wv.at[me], wv)
    g1(1)
    g_ref[...] = group_matrix()
    for r in (xa, xb, xf, d3, dp):
        clear_edges(r)
    turned(lat_t, lat)
    turned(hint_t, hint)

    def latent_at(i):
        return lat[rows(i, TILE), :].astype(F32)

    def mixed_at(i):
        return latent_at(i) + hint[rows(i, TILE), :].astype(F32)

    def p_at(i):
        return p[rows(i, TILE), :]

    g2(0)
    spread_wait(0, wv)
    pick = lax.broadcasted_iota(jnp.int32, (C, 20), 0) == me * 20 + lax.broadcasted_iota(jnp.int32, (C, 20), 1)
    mine = jnp.dot(stacked(wv).astype(BF), pick.astype(F32).astype(BF), preferred_element_type=F32).astype(BF)
    pre = jnp.dot(mine, tw[...], preferred_element_type=F32)
    for e in range(16):
        pb[e] = pre[:, e * 80 : (e + 1) * 80]
    pr[me] = pb[me]
    spread(1, lambda to: pb.at[to], pr)
    turned(sg_t, sg)
    normed_silu(mixed_at, xa, g_ref)
    g3(0)
    g2(1)
    g1(2)
    spread_wait(1, pr)
    total = pr[0]
    for s in range(1, 16):
        total = total + pr[s]
    em[...] = (total * jax.nn.sigmoid(total)).astype(BF).astype(F32)
    emb = em[...].astype(BF)
    row_f = jnp.dot(emb, fe[...], preferred_element_type=F32)
    row_t = jnp.dot(emb, te[...], preferred_element_type=F32)
    both = jnp.concatenate([row_f, row_t], axis=1)
    for s in range(16):
        rb[s] = both[s : s + 1, :]
    rr[me] = rb[me]
    spread(2, lambda to: rb.at[to], rr)
    g4(0)
    normed_silu(latent_at, xf, g_ref)
    g3(1)
    g2(2)
    g1(3)
    spread_wait(2, rr)
    row = rr[0]
    for s in range(1, 16):
        row = row + rr[s]
    frozen_row, train_row = row[:, 0:C], row[:, C : 2 * C]
    g5(0, w1)
    for d in range(16):
        for h in range(2):
            wz[d * 20 + h * 10 : d * 20 + (h + 1) * 10, :] = ga[d % 2, d // 2, HALF:HALF_Z, h * C : (h + 1) * C]

    def put_p(e):
        def write(m, acc):
            p[rows(m, MT), :] = acc + e

        return write

    conv(xa, w1, put_p(train_row))
    g4(1)
    g3(2)
    g2(3)

    def dc_body(i, c):
        d = lax.dot_general(sg[rows(i, TILE), :], wz[...], (((1,), (1,)), ((), ())), preferred_element_type=F32)
        d = d.astype(BF).astype(F32)
        dp[rows(i, TILE, COLS), :] = d.astype(BF)
        put_shifted(d, d3, i, -1)
        return c

    lax.fori_loop(0, STEPS, dc_body, 0)
    mean, inverse = stats(p_at, g_ref)

    def y_body(i, c):
        v = (p_at(i) - mean) * inverse
        y1[rows(i, TILE), :] = v
        put_shifted(v * jax.nn.sigmoid(v), xb, i, 1)
        return c

    lax.fori_loop(0, STEPS, y_body, 0)
    g5(1, w2)
    g4(2)
    g3(3)

    def write_control(m, acc):
        mixed = lat[rows(m, MT), :].astype(F32) + hint[rows(m, MT), :].astype(F32)
        ctl[rows(m, MT), :] = (mixed + acc).astype(BF)

    conv(xb, w2, write_control)
    g4(3)

    sums = (
        (out_a, in_a, xp_a, xq_a, zb_a, cur_a, got_a),
        (out_b, in_b, xp_b, xq_b, zb_b, cur_b, got_b),
    )

    def packed(n):
        out = sums[n][0]
        for d in range(16):
            for h in range(2):
                out[d % 2, d // 2, 0:HALF, h * C : (h + 1) * C] = dw[
                    d * 180 + h * HALF : d * 180 + (h + 1) * HALF, :
                ]

    def r1(n):
        out, inn = sums[n][:2]
        send(out.at[oc], inn, r_send.at[n, 0], r_recv.at[n, 0], mate)

    def r2(n):
        out, inn, xp = sums[n][:3]
        landed(inn, r_recv.at[n, 0])
        for h in range(2):
            j = xo * 2 + h
            add_into(out.at[core, j], inn.at[j])
            send(out.at[core, j], xp.at[h], r_send.at[n, 1 + h], r_recv.at[n, 1 + h], (right, left)[h])
        for xs in (xr, xl, x):
            for h in range(2):
                add_into(out.at[core, xs * 2 + h], inn.at[xs * 2 + h])

    def r3(n):
        out, _, xp, xq = sums[n][:4]
        for h in range(2):
            landed(xp.at[h], r_recv.at[n, 1 + h])
            xs = (xr, xl)[h]
            add_into(out.at[core, xs * 2 + h], xp.at[h])
            send(out.at[core, pl.ds(xs * 2, 2)], xq.at[h], r_send.at[n, 3 + h], r_recv.at[n, 3 + h], (right, left)[h])

    def r4(n):
        out, _, _, xq, zb = sums[n][:5]
        landed(xq.at[0], r_recv.at[n, 3])
        landed(xq.at[1], r_recv.at[n, 4])
        add_into(out.at[core, x * 2 + oh], xq.at[0, oh], xq.at[1, oh])
        send(out.at[core, x * 2 + oh], zb, r_send.at[n, 5], r_recv.at[n, 5], z_b)
        add_into(out.at[core, x * 2 + zh], xq.at[0, zh], xq.at[1, zh])

    def r5(n):
        out, _, _, _, zb, cur, got = sums[n]
        size = zb.shape[0]
        landed(zb, r_recv.at[n, 5])
        cur[0, 0:size, :] = (out[core, x * 2 + zh].astype(F32) + zb[...].astype(F32)).astype(BF)
        send(cur.at[0], got.at[0], r_send.at[n, 6], r_recv.at[n, 6], z_a)

    def r6(n, k):
        cur, got = sums[n][5:7]
        landed(got.at[k], r_recv.at[n, 6 + k])
        cur[k + 1] = (cur[k].astype(F32) + got[k].astype(F32)).astype(BF)
        send(cur.at[k + 1], got.at[k + 1], r_send.at[n, 7 + k], r_recv.at[n, 7 + k], (y_a, y_b)[k])

    def conv_grad_dots(x3):
        for b in range(3):
            lhs = x3[COLS : COLS + POS, b * C : (b + 1) * C]
            for a in range(3):
                k = 3 * a + b
                t = lax.dot_general(
                    lhs, dp[128 - 64 * a : 128 - 64 * a + POS, :], (((0,), (0,)), ((), ())),
                    preferred_element_type=F32,
                )
                dw[k * C : (k + 1) * C, :] = t.astype(BF)

    dz = lax.dot_general(ctl[...], sg[...], (((0,), (0,)), ((), ())), preferred_element_type=F32)
    for d in range(16):
        for h in range(2):
            at = d * 20 + h * 10
            out_a[d % 2, d // 2, HALF:HALF_Z, h * C : (h + 1) * C] = dz[at : at + 10, :].astype(BF)
    conv_grad_dots(xb)
    packed(0)
    r1(0)
    g5(2, v1)

    def write_da(m, acc):
        p[rows(m, MT), :] = acc

    conv_back(d3, w2, write_da)
    r2(0)
    zero = jnp.zeros((8, C), F32)

    def dy_body(i, s):
        v = y1[rows(i, TILE), :]
        sig = jax.nn.sigmoid(v)
        dy = p_at(i) * sig * (1.0 + v * (1.0 - sig))
        p[rows(i, TILE), :] = dy
        return s[0] + fold(dy), s[1] + fold(dy * v)

    s1, s2 = lax.fori_loop(0, STEPS, dy_body, (zero, zero))
    m1, m2 = group_mean(s1, g_ref), group_mean(s2, g_ref)

    def dp_body(i, s):
        d = (p_at(i) - m1 - y1[rows(i, TILE), :] * m2) * inverse
        dp[rows(i, TILE, COLS), :] = d.astype(BF)
        return s + fold(d)

    es[me] = jnp.sum(lax.fori_loop(0, STEPS, dp_body, zero), axis=0, keepdims=True)
    spread(3, lambda to: es.at[me], es)
    r3(0)
    conv_grad_dots(xa)
    packed(1)
    r1(1)
    r4(0)
    g5(3, v2)
    conv(xf, v1, put_p(frozen_row))
    r2(1)
    r5(0)
    spread_wait(3, es)
    de = lax.dot_general(
        em[...], stacked(es), (((0,), (0,)), ((), ())), preferred_element_type=F32, precision=EXACT
    )
    for h in range(2):
        cur_b[0, HALF : HALF + 40, h * C : (h + 1) * C] = de[h * 40 : (h + 1) * 40, :].astype(BF)
    normed_silu(p_at, xf, g_ref)
    r3(1)
    r6(0, 0)

    def write_skip(m, acc):
        out = lat[rows(m, MT), :].astype(F32) + acc
        out = out + jnp.dot(ctl[rows(m, MT), :], wz[...], preferred_element_type=F32)
        skip[:, pl.ds(pl.multiple_of(m * MT, MT), MT)] = out.T.astype(BF)

    conv(xf, v2, write_skip)
    r4(1)
    r6(0, 1)
    r5(1)
    r6(1, 0)
    r6(1, 1)
    landed(got_a.at[2], r_recv.at[0, 8])
    tot_a = cur_a[2].astype(F32) + got_a[2].astype(F32)
    sq = jnp.sum(tot_a * tot_a, axis=0, keepdims=True)
    landed(got_b.at[2], r_recv.at[1, 8])
    tot_b = cur_b[2].astype(F32) + got_b[2].astype(F32)
    sq = sq + jnp.sum(tot_b * tot_b, axis=0, keepdims=True)
    nr[me] = jnp.broadcast_to(jnp.sum(sq, axis=1, keepdims=True), (1, 128))
    spread(4, lambda to: nr.at[me], nr)
    spread_wait(4, nr)
    total = nr[0]
    for s in range(1, 16):
        total = total + nr[s]
    norm = jnp.sqrt(total[:, 0:1] + 1e-06)
    scale = jnp.minimum(1.0, clip_limit / norm)
    onorm[...] = norm
    for h in range(2):
        c = slice(h * C, (h + 1) * C)
        o2[h * HALF : (h + 1) * HALF, :] = tot_a[0:HALF, c] * scale
        oz[h * 10 : (h + 1) * 10, :] = tot_a[HALF:HALF_Z, c] * scale
        o1[h * HALF : (h + 1) * HALF, :] = tot_b[0:HALF, c] * scale
        oe[h * 40 : (h + 1) * 40, :] = tot_b[HALF : HALF + 40, c] * scale
    for c in started:
        c.wait_send()
    spread_sent(0, lambda to: wv.at[me], wv)
    spread_sent(1, lambda to: pb.at[to], pr)
    spread_sent(2, lambda to: rb.at[to], rr)
    spread_sent(3, lambda to: es.at[me], es)
    spread_sent(4, lambda to: nr.at[me], nr)


def vm(shape, dtype=BF):
    return pltpu.VMEM(shape, dtype)


SCRATCH = [
    vm((POS, C)), vm((POS, C)), vm((POS, C)), vm((C, C), F32),
    vm((POS + 2 * COLS, 3 * C)), vm((POS + 2 * COLS, 3 * C)), vm((POS + 2 * COLS, 3 * C)),
    vm((POS + 2 * COLS, 3 * C)), vm((POS + 2 * COLS, C)),
    vm((POS, C), F32), vm((POS, C), F32), vm((POS, C)), vm((9 * C, C)),
    vm((9 * C, C)), vm((9 * C, C)), vm((9 * C, C)), vm((9 * C, C)), vm((C, C)),
    vm((2, 8, HALF_Z, 2 * C)), vm((2, 8, HALF, 2 * C)), vm((2, 8, HALF, 2 * C)), vm((2, 8, HALF, 2 * C)),
    vm((16, 1, C), F32), vm((16, 16, 80), F32), vm((16, 16, 80), F32), vm((16, 1, 2 * C), F32),
    vm((16, 1, 2 * C), F32), vm((16, 80), F32), vm((16, 1, C), F32),
    vm((16, 1, 128), F32),
    vm((2, 8, HALF_Z, 2 * C)), vm((2, 8, HALF, 2 * C)),
    vm((8, HALF_Z, 2 * C)), vm((8, HALF, 2 * C)),
    vm((2, HALF_Z, 2 * C)), vm((2, HALF, 2 * C)),
    vm((2, 2, HALF_Z, 2 * C)), vm((2, 2, HALF, 2 * C)),
    vm((HALF_Z, 2 * C)), vm((HALF, 2 * C)),
    vm((3, HALF_Z, 2 * C)), vm((3, HALF + 40, 2 * C)),
    vm((3, HALF_Z, 2 * C)), vm((3, HALF + 40, 2 * C)),
    pltpu.SemaphoreType.DMA((4, 16)), pltpu.SemaphoreType.DMA((4, 16)),
    pltpu.SemaphoreType.DMA((5, 16)), pltpu.SemaphoreType.DMA((5, 16)),
    pltpu.SemaphoreType.DMA((2, 9)), pltpu.SemaphoreType.DMA((2, 9)),
]


def wave_of(timestep):
    half = C // 2
    freqs = jnp.exp(-math.log(10000.0) * jnp.arange(half).astype(F32) / half)
    angles = timestep.astype(F32)[:, None] * freqs[None, :]
    return jnp.concatenate([jnp.cos(angles), jnp.sin(angles)], axis=1).astype(BF).astype(F32)


def shards(
    latent, hint, timestep, skip_grad, frozen_one, frozen_two, time_weight, frozen_emb,
    train_one, train_two, train_emb, zero_weight,
):
    spec = pl.BlockSpec(memory_space=pltpu.VMEM)
    skip, g1, g2, ge, gz, norm = pl.pallas_call(
        kernel,
        out_shape=(
            jax.ShapeDtypeStruct((C, POS), BF),
            jax.ShapeDtypeStruct((180, C), F32),
            jax.ShapeDtypeStruct((180, C), F32),
            jax.ShapeDtypeStruct((80, C), F32),
            jax.ShapeDtypeStruct((20, C), F32),
            jax.ShapeDtypeStruct((1, 1), F32),
        ),
        in_specs=[spec] * 12,
        out_specs=[spec] * 6,
        scratch_shapes=SCRATCH,
        compiler_params=pltpu.CompilerParams(
            vmem_limit_bytes=67043328, collective_id=0, has_side_effects=True
        ),
    )(
        latent[0].T, hint[0].T, skip_grad[0].T, wave_of(timestep), frozen_one, frozen_two, time_weight, frozen_emb,
        train_one, train_two, train_emb, zero_weight,
    )
    return (skip.T[None], g1, g2, ge, gz, norm[0, 0])


def solution(mesh):
    data, rows_of = P(("dp", "fsdp"), None, None), P("fsdp", None)
    return jax.shard_map(
        shards,
        mesh=mesh,
        in_specs=(data, data, P(("dp", "fsdp")), data) + (rows_of,) * 8,
        out_specs=(data, rows_of, rows_of, rows_of, rows_of, P()),
        check_vma=False,
    )
```

time: 440 us -> 127 us (0.29); the launches traced: 435 us -> 126 us
  waiting for transfers between devices: 183 us -> 0 us
  Pallas kernels: 48.5 us -> 117 us
  local copies, waits for them, and re-layouts: 69.9 us -> 5.46 us
  blocking collectives: 56.7 us -> 0 us
  other arithmetic: 30.9 us -> 0.68 us
  starting transfers between devices: 25 us -> 0 us
  between operations: 19.3 us -> 3.09 us
    reduce_scatter x1 -> x0, waiting for transfers between devices: 78.7 us -> none  [sum_packed(): lax.psum_scatter(lines, axis, tiled=True).reshape(-1)]
    pallas_call x1, Pallas kernels: 48.5 us -> 117 us  [shards(): pl.pallas_call(kernel, out_shape=(jax.ShapeDtypeStruct((C, POS), BF), jax...]
    all_gather x2 -> x0, waiting for transfers between devices: 64.5 us -> none  [the longest x1 64.5 us: gather_packed(): lines, at, gathered = (lax.all_gather(vector, axis), 0, [])]
    all_gather x2 -> x0, blocking collectives: 56.7 us -> none  [the longest x1 30.6 us: shards(): lax.all_gather(time_weight, 'fsdp', axis=0, tiled=True)]
    all_to_all x5 -> x0, waiting for transfers between devices: 39.6 us -> none  [sent_to_all(): return lax.all_to_all(copies, axis, split_axis=0, concat_axis=0, tiled=True)]
    all_to_all x5 -> x0, starting transfers between devices: 24.9 us -> none  [sent_to_all(): return lax.all_to_all(copies, axis, split_axis=0, concat_axis=0, tiled=True)]
    another operation x7 -> x0, local copies, waits for them, and re-layouts: 23 us -> none  [the longest x4 11.8 us: laid_out(): tiles.reshape(*shape[:dim], shape[dim] * shape[dim + 1], *shape[dim + 2:])]
    concatenate x3 -> x0, other arithmetic: 19.6 us -> none  [the longest x1 19.5 us: sum_packed(): lines = jnp.concatenate([b.reshape(size, -1) for b in tiles], axis=1)]
  transfers between devices with their start and end apart: 8 -> 0, of which waited for: 7 -> 0; matrix products, arithmetic and copies ran while one was open for 7% -> 0% of each run, Pallas kernels for 0% -> 0%
where the time goes in v1:
time: 127 us; the launch traced here: 126 us
  Pallas kernels  117 us (92%)
  local copies, waits for them, and re-layouts  5.46 us (4%)
  between operations  3.09 us (2%)
    pallas_call x1, Pallas kernels, shards(): pl.pallas_call(kernel, out_shape=(jax.ShapeDtypeStruct((C, POS), BF), jax...  117 us
    unnamed x13, local copies, waits for them, and re-layouts  5.45 us

profile of v1, /device:TPU:1, one launch (start us, length us, event | category | flops | bytes accessed | tf_op | source)
XLA Modules:
  0.0 126.4 jit_solution(8017841307562111523)
XLA Ops:
  1.4 0.6 maximum_convert_fusion.wave
  2.0 117.1 %shard_map.163 = (bf16[320,1024]{1,0:T(8,128)(2,1)}, f32[180,320]{1,0:T(8,128)}, f32[180,320]{1,0:T(8,128)}, f32[80,320]{1,0:T(8,128)}, f32[20,320]{1,0:T(8,128)}, /*index=5*/f32[1,1]{1,0:T(1,128)}) custom-call(bf16[320,1024]{1,0:T(8,128)(2,1)} %bitcast.15, bf16[320,1024]{1,0:T(8,128)(2,1)} %bitcast.16, bf16[320,1024]{1,0:T(8,128)(2,1)} %bitcast.17, ...), custom_call_target="tpu_custom_call" | custom-call | tf_op jit(solution)/shard_map/pallas_call | solution.py:594
  119.1 0.0 copy-start.1
  119.1 2.0 %copy.25 = bf16[1,1024,320]{1,2,0:T(8,128)(2,1)} copy(bf16[1,1024,320]{1,2,0:T(8,128)(2,1)} %bitcast.14) | data formatting | bytes 1310720
  121.2 0.0 copy-done.1
  121.2 0.0 copy-start
  121.2 0.7 copy.26
  121.9 0.3 copy-done
  122.2 0.0 copy-start.2
  122.2 0.7 copy.27
  122.9 0.3 copy-done.2
  123.2 0.0 copy-start.3
  123.2 0.6 copy.28
  123.9 0.1 copy-done.3
  124.0 0.6 copy.29
  (3 shorter events, 0.1 us)
Async XLA Ops:
  119.1 2.0 %copy-start.1 = (f32[180,320]{1,0:T(8,128)S(1)}, f32[180,320]{1,0:T(8,128)}, u32[]{:S(2)}) copy-start(f32[180,320]{1,0:T(8,128)} %get-tuple-element.27) | copy-start | bytes 691204
  121.2 1.1 copy-start
  122.2 1.0 copy-start.2
  123.2 0.8 copy-start.3

commit v2 on v1

v2 whole, which is shorter than its diff:
```python
import math

import jax
import jax.numpy as jnp
from jax import lax
from jax.experimental import pallas as pl
from jax.experimental.pallas import tpu as pltpu
from jax.sharding import PartitionSpec as P

COLS = 64
POS = 1024
C = 320
TEMB = 1280
TILE = 128
STEPS = POS // TILE
MT = 256
HALF = 90
AT = 96
F32 = jnp.float32
BF = jnp.bfloat16
EPS = 1e-05
COUNT = POS * 10.0
clip_limit = 1.0
EXACT = lax.Precision.HIGHEST
MESH = pl.DeviceIdType.MESH


def rows(i, size, base=0):
    return pl.ds(pl.multiple_of(i * size + base, 16), size)


def group_matrix():
    r = lax.broadcasted_iota(jnp.int32, (C, C), 0)
    c = lax.broadcasted_iota(jnp.int32, (C, C), 1)
    return ((r * 6554) // 65536 == (c * 6554) // 65536).astype(F32).astype(BF)


def fold(x):
    return x.reshape(TILE // 8, 8, C).sum(axis=0)


def group_mean(part, g_ref):
    high = part.astype(BF)
    rest = part - high.astype(F32)
    mid = rest.astype(BF)
    low = (rest - mid.astype(F32)).astype(BF)
    split = jnp.concatenate([high, mid, low], axis=0)
    total = jnp.dot(split, g_ref[...], preferred_element_type=F32)
    return jnp.sum(total, axis=0, keepdims=True) * (1.0 / COUNT)


def stats(read, g_ref):
    zero = jnp.zeros((8, C), F32)
    mean = group_mean(lax.fori_loop(0, STEPS, lambda i, s: s + fold(read(i)), zero), g_ref)

    def square(i, s):
        d = read(i) - mean
        return s + fold(d * d)

    var = group_mean(lax.fori_loop(0, STEPS, square, zero), g_ref)
    return mean, lax.rsqrt(var + EPS)


def put_shifted(x, ref, i, order):
    j = lax.broadcasted_iota(jnp.int32, (TILE, C), 0) % COLS
    before = jnp.where(j == 0, 0.0, pltpu.roll(x, 1, 0)).astype(BF)
    after = jnp.where(j == COLS - 1, 0.0, pltpu.roll(x, TILE - 1, 0)).astype(BF)
    mid = x.astype(BF)
    parts = (before, mid, after) if order > 0 else (after, mid, before)
    ref[rows(i, TILE, COLS), :] = jnp.concatenate(parts, axis=1)


def clear_edges(ref):
    z = jnp.zeros((COLS, ref.shape[1]), ref.dtype)
    ref[0:COLS, :] = z
    ref[COLS + POS : 2 * COLS + POS, :] = z


def normed_silu(read, x3, g_ref):
    mean, inverse = stats(read, g_ref)

    def body(i, c):
        y = (read(i) - mean) * inverse
        put_shifted(y * jax.nn.sigmoid(y), x3, i, 1)
        return c

    lax.fori_loop(0, STEPS, body, 0)


def conv(x3, w_ref, write, first=0, last=POS // MT):
    def body(m, c):
        acc = None
        for a in range(3):
            t = jnp.dot(
                x3[rows(m, MT, a * COLS), :], w_ref[a * 960 : (a + 1) * 960, :], preferred_element_type=F32
            )
            acc = t if acc is None else acc + t
        write(m, acc)
        return c

    lax.fori_loop(first, last, body, 0)


def conv_back(d3, w_ref, write, first=0, last=POS // MT):
    def body(m, c):
        acc = None
        for a in range(3):
            for b in range(3):
                k = 3 * a + b
                t = lax.dot_general(
                    d3[rows(m, MT, (2 - a) * COLS), b * C : (b + 1) * C],
                    w_ref[k * C : (k + 1) * C, :],
                    (((1,), (1,)), ((), ())),
                    preferred_element_type=F32,
                )
                acc = t if acc is None else acc + t
        write(m, acc)
        return c

    lax.fori_loop(first, last, body, 0)


def turned(src, dst):
    def body(i, c):
        cols = pl.ds(pl.multiple_of(i * TILE, TILE), TILE)
        dst[rows(i, TILE), :] = src[:, cols].astype(F32).T.astype(BF)
        return c

    lax.fori_loop(0, STEPS, body, 0)


def paired(ref, dst, at, size):
    dst[at : at + size, 0:C] = ref[0:size, :]
    dst[at : at + size, C : 2 * C] = ref[size : 2 * size, :]


def add_into(dst, *others):
    total = dst[...].astype(F32)
    for o in others:
        total = total + o[...].astype(F32)
    dst[...] = total.astype(BF)


def kernel(
    lat_h, hint_h, sg_h, wave_h, f1_h, f2_h, tw_h, fe_h, t1_h, t2_h, te_h, zw_h,
    skip_h, oa_h, ob_h, onorm_h,
    lat_t, hint_t, sg_t, wave, f1, f2, tw, fe, t1, t2, te, zw, skip, oa, ob, onorm, i_sem, o_sem,
    lat, hint, sg, g_ref, xa, xb, xf, d3, dp, dq, y1, p, ctl, dw,
    w1, w2, v1, v2, wz,
    ga, gb, gc, gd, gz,
    wv, pb, pr, rb, rr, em, es, nr,
    out_a, out_b, in_a, in_b, xp_a, xp_b, xq_a, xq_b, zb_a, zb_b, cur_a, cur_b, got_a, got_b,
    g_send, g_recv, e_send, e_recv, r_send, r_recv,
):
    me_dp, me = lax.axis_index("dp"), lax.axis_index("fsdp")
    core, zh, x = lax.rem(me, 2), lax.rem(me // 2, 2), me // 4
    y, zl = me_dp // 2, lax.rem(me_dp, 2)
    oc, oh, ol = 1 - core, 1 - zh, 1 - zl
    xr, xl, xo = lax.rem(x + 1, 4), lax.rem(x + 3, 4), lax.rem(x + 2, 4)
    y_near = y + 1 - 2 * lax.rem(y, 2)
    right = (me_dp, xr * 4 + zh * 2 + core)
    left = (me_dp, xl * 4 + zh * 2 + core)
    mate = (me_dp, x * 4 + zh * 2 + oc)
    z_b = (y * 2 + ol, x * 4 + oh * 2 + core)
    z_a = (y * 2 + ol, me)
    y_a = (y_near * 2 + zl, me)
    y_b = ((3 - y) * 2 + zl, me)

    def send(src, dst, ssem, rsem, to):
        pltpu.make_async_remote_copy(
            src_ref=src, dst_ref=dst, send_sem=ssem, recv_sem=rsem, device_id=to, device_id_type=MESH
        ).start()

    def landed(ref, rsem):
        pltpu.make_async_remote_copy(
            src_ref=ref, dst_ref=ref, send_sem=rsem, recv_sem=rsem, device_id=mate, device_id_type=MESH
        ).wait_recv()

    barrier = pltpu.get_barrier_semaphore()

    def greet(k, c):
        pl.semaphore_signal(barrier, inc=1, device_id=(me_dp, lax.rem(me + k, 16)), device_id_type=MESH)
        return c

    lax.fori_loop(1, 16, greet, 0)
    for to in (z_b, z_a, y_a, y_b):
        pl.semaphore_signal(barrier, inc=1, device_id=to, device_id_type=MESH)
    from_hbm = {}
    loads = (
        ("t1", t1_h, t1), ("zw", zw_h, zw), ("wave", wave_h, wave), ("t2", t2_h, t2), ("lat", lat_h, lat_t),
        ("f1", f1_h, f1), ("f2", f2_h, f2), ("tw", tw_h, tw), ("hint", hint_h, hint_t), ("sg", sg_h, sg_t),
        ("fe", fe_h, fe), ("te", te_h, te),
    )
    for n, (name, src, dst) in enumerate(loads):
        from_hbm[name] = pltpu.make_async_copy(src, dst, i_sem.at[n])
        from_hbm[name].start()
    gathered = (ga, gb, gc, gd, gz)
    own = x * 2 + zh
    from_hbm["t1"].wait()
    from_hbm["zw"].wait()
    paired(t1, ga.at[core, own], 0, HALF)
    paired(zw, gz.at[core, own], 0, 10)
    from_hbm["wave"].wait()
    wv[me] = wave[...]
    from_hbm["t2"].wait()
    paired(t2, gb.at[core, own], 0, HALF)
    pl.semaphore_wait(barrier, 19)

    parts = ((4, 0, 8, 10), (0, 0, 24, 48), (0, 48, 72, HALF), (1, 0, 48, HALF), (2, 0, 48, HALF), (3, 0, 48, HALF))

    def block(u, j):
        w, lo, _, hi = parts[u]
        return gathered[w].at[core, j, pl.ds(lo, hi - lo)]

    def low(u, j):
        w, lo, mid, _ = parts[u]
        return gathered[w].at[core, j, pl.ds(lo, mid - lo)]

    def high(u, j):
        w, _, mid, hi = parts[u]
        return gathered[w].at[core, j, pl.ds(mid, hi - mid)]

    def pass_on(u, j):
        send(block(u, j), block(u, j), g_send.at[u, 0], g_recv.at[u, 8], mate)

    def g1(u):
        b = block(u, own)
        send(b, b, g_send.at[u, 1], g_recv.at[u, 0], right)
        send(b, b, g_send.at[u, 1], g_recv.at[u, 1], left)
        pass_on(u, own)

    def g1z(u):
        b = block(u, own)
        send(b, b, g_send.at[u, 1], g_recv.at[u, 2], z_b)

    def g2(u):
        jl, jr, jz = xl * 2 + zh, xr * 2 + zh, x * 2 + oh
        landed(block(u, jl), g_recv.at[u, 0])
        send(low(u, jl), low(u, jl), g_send.at[u, 1], g_recv.at[u, 3], right)
        landed(block(u, jr), g_recv.at[u, 1])
        send(high(u, jr), high(u, jr), g_send.at[u, 1], g_recv.at[u, 4], left)
        landed(block(u, jz), g_recv.at[u, 2])
        send(block(u, jz), block(u, jz), g_send.at[u, 1], g_recv.at[u, 5], right)
        send(block(u, jz), block(u, jz), g_send.at[u, 1], g_recv.at[u, 6], left)
        pass_on(u, jl)
        pass_on(u, jr)
        pass_on(u, jz)

    def g3(u):
        jo, jl, jr = xo * 2 + zh, xl * 2 + oh, xr * 2 + oh
        landed(low(u, jo), g_recv.at[u, 3])
        landed(high(u, jo), g_recv.at[u, 4])
        send(block(u, jo), block(u, jo), g_send.at[u, 1], g_recv.at[u, 7], z_b)
        pass_on(u, jo)
        landed(block(u, jl), g_recv.at[u, 5])
        pass_on(u, jl)
        landed(block(u, jr), g_recv.at[u, 6])
        pass_on(u, jr)

    def g4(u):
        jz = xo * 2 + oh
        landed(block(u, jz), g_recv.at[u, 7])
        pass_on(u, jz)

    def g5(u):
        w, lo, _, hi = parts[u]
        landed(gathered[w].at[oc, :, pl.ds(lo, hi - lo)], g_recv.at[u, 8])

    def sent(ref, ssem):
        pltpu.make_async_remote_copy(
            src_ref=ref, dst_ref=ref, send_sem=ssem, recv_sem=ssem, device_id=mate, device_id_type=MESH
        ).wait_send()

    def g_sent(u):
        w, lo, _, hi = parts[u]
        r = pl.ds(lo, hi - lo)
        sent(gathered[w].at[core, :, r], g_send.at[u, 0])
        sent(gathered[w].at[core, pl.ds(0, 7), r], g_send.at[u, 1])

    def unpacked(w, full):
        g = gathered[w]
        for d in range(16):
            for h in range(2):
                full[d * 180 + h * HALF : d * 180 + (h + 1) * HALF, :] = g[
                    d % 2, d // 2, 0:HALF, h * C : (h + 1) * C
                ]

    def spread(n, src_of, dst):
        def body(k, c):
            to = lax.rem(me + k, 16)
            pltpu.make_async_remote_copy(
                src_ref=src_of(to), dst_ref=dst.at[me], send_sem=e_send.at[n], recv_sem=e_recv.at[n],
                device_id=(me_dp, to), device_id_type=MESH,
            ).start()
            return c

        lax.fori_loop(1, 16, body, 0)

    def spread_wait(n, dst):
        landed(dst.at[pl.ds(0, 15)], e_recv.at[n])

    def spread_sent(n, dst):
        sent(dst.at[pl.ds(0, 15)], e_send.at[n])

    def stacked(ref):
        return jnp.concatenate([ref[s] for s in range(16)], axis=0)

    def sum_of(ref):
        total = ref[0]
        for k in range(1, 16):
            total = total + ref[k]
        return total

    chains = (
        (out_b, in_b, xp_b, xq_b, zb_b, cur_b, got_b, 0, 48, 48),
        (out_b, in_b, xp_b, xq_b, zb_b, cur_b, got_b, 48, AT, AT + 40),
        (out_a, in_a, xp_a, xq_a, zb_a, cur_a, got_a, 0, 48, 48),
        (out_a, in_a, xp_a, xq_a, zb_a, cur_a, got_a, 48, AT + 16, AT + 16),
    )

    def packed(out):
        for d in range(16):
            for h in range(2):
                out[d % 2, d // 2, 0:HALF, h * C : (h + 1) * C] = dw[
                    d * 180 + h * HALF : d * 180 + (h + 1) * HALF, :
                ]

    def step(n, k):
        out, inn, xp, xq, zb, cur, got, lo, hi, far = chains[n]
        r = pl.ds(lo, hi - lo)
        wide = pl.ds(lo, far - lo)
        if k == 1:
            send(out.at[oc, :, r], inn.at[:, r], r_send.at[n, 0], r_recv.at[n, 0], mate)
        elif k == 2:
            landed(inn.at[:, r], r_recv.at[n, 0])
            for h in range(2):
                j = xo * 2 + h
                add_into(out.at[core, j, r], inn.at[j, r])
                send(out.at[core, j, r], xp.at[h, r], r_send.at[n, 1], r_recv.at[n, 1 + h], (right, left)[h])
            for xs in (xr, xl, x):
                for h in range(2):
                    add_into(out.at[core, xs * 2 + h, r], inn.at[xs * 2 + h, r])
        elif k == 3:
            for h in range(2):
                landed(xp.at[h, r], r_recv.at[n, 1 + h])
                xs = (xr, xl)[h]
                add_into(out.at[core, xs * 2 + h, r], xp.at[h, r])
                send(
                    out.at[core, pl.ds(xs * 2, 2), r], xq.at[h, :, r], r_send.at[n, 1], r_recv.at[n, 3 + h],
                    (right, left)[h],
                )
        elif k == 4:
            landed(xq.at[0, :, r], r_recv.at[n, 3])
            landed(xq.at[1, :, r], r_recv.at[n, 4])
            add_into(out.at[core, x * 2 + oh, r], xq.at[0, oh, r], xq.at[1, oh, r])
            send(out.at[core, x * 2 + oh, r], zb.at[r], r_send.at[n, 1], r_recv.at[n, 5], z_b)
            add_into(out.at[core, x * 2 + zh, r], xq.at[0, zh, r], xq.at[1, zh, r])
        elif k == 5:
            landed(zb.at[r], r_recv.at[n, 5])
            cur[0, lo:hi, :] = (out[core, x * 2 + zh, lo:hi, :].astype(F32) + zb[lo:hi, :].astype(F32)).astype(BF)
            send(cur.at[0, wide], got.at[0, wide], r_send.at[n, 2], r_recv.at[n, 6], z_a)
        elif k < 8:
            m = k - 6
            landed(got.at[m, wide], r_recv.at[n, 6 + m])
            cur[m + 1, lo:far, :] = (cur[m, lo:far, :].astype(F32) + got[m, lo:far, :].astype(F32)).astype(BF)
            send(
                cur.at[m + 1, wide], got.at[m + 1, wide], r_send.at[n, 2], r_recv.at[n, 7 + m], (y_a, y_b)[m]
            )
        else:
            landed(got.at[2, wide], r_recv.at[n, 8])

    def step_sent(n):
        out, inn, xp, xq, zb, cur, got, lo, hi, far = chains[n]
        sent(inn.at[:, pl.ds(lo, hi - lo)], r_send.at[n, 0])
        sent(inn.at[pl.ds(0, 7), pl.ds(lo, hi - lo)], r_send.at[n, 1])
        sent(got.at[:, pl.ds(lo, far - lo)], r_send.at[n, 2])

    def grad_dots(x3, cot, b):
        lhs = x3[COLS : COLS + POS, b * C : (b + 1) * C]
        for a in range(3):
            k = 3 * a + b
            t = lax.dot_general(
                lhs, cot[128 - 64 * a : 128 - 64 * a + POS, :], (((0,), (0,)), ((), ())), preferred_element_type=F32
            )
            dw[k * C : (k + 1) * C, :] = t.astype(BF)

    def put_p(m, acc):
        p[rows(m, MT), :] = acc

    def latent_at(i):
        return lat[rows(i, TILE), :].astype(F32)

    def mixed_at(i):
        return latent_at(i) + hint[rows(i, TILE), :].astype(F32)

    for u in range(3):
        g1(u)
        g1z(u)
    spread(0, lambda to: wv.at[me], wv)
    from_hbm["f1"].wait()
    paired(f1, gc.at[core, own], 0, HALF)
    from_hbm["f2"].wait()
    paired(f2, gd.at[core, own], 0, HALF)
    from_hbm["lat"].wait()
    turned(lat_t, lat)
    from_hbm["hint"].wait()
    turned(hint_t, hint)
    g_ref[...] = group_matrix()
    for r in (xa, xb, xf, d3, dp, dq):
        clear_edges(r)
    for out, top in ((out_a, AT + 16), (out_b, AT)):
        out[:, :, 80:top, :] = jnp.zeros((2, 8, top - 80, 2 * C), BF)
    from_hbm["sg"].wait()
    turned(sg_t, sg)
    g2(0)
    g2(1)
    normed_silu(mixed_at, xa, g_ref)
    g2(2)
    g3(0)
    spread_wait(0, wv)
    from_hbm["tw"].wait()
    pick = lax.broadcasted_iota(jnp.int32, (C, 20), 0) == me * 20 + lax.broadcasted_iota(jnp.int32, (C, 20), 1)
    mine = jnp.dot(stacked(wv).astype(BF), pick.astype(F32).astype(BF), preferred_element_type=F32).astype(BF)
    pre = jnp.dot(mine, tw[...], preferred_element_type=F32)
    for e in range(16):
        pb[e] = pre[:, e * 80 : (e + 1) * 80]
    pr[me] = pb[me]
    spread(1, lambda to: pb.at[to], pr)
    g1(3)
    g3(1)
    normed_silu(latent_at, xf, g_ref)
    g3(2)
    g1z(3)
    g4(0)
    g5(0)
    for d in range(16):
        for h in range(2):
            wz[d * 20 + h * 10 : d * 20 + (h + 1) * 10, :] = gz[d % 2, d // 2, :, h * C : (h + 1) * C]

    def dc_body(i, c):
        d = lax.dot_general(sg[rows(i, TILE), :], wz[...], (((1,), (1,)), ((), ())), preferred_element_type=F32)
        d = d.astype(BF).astype(F32)
        dp[rows(i, TILE, COLS), :] = d.astype(BF)
        put_shifted(d, d3, i, -1)
        return c

    lax.fori_loop(0, STEPS, dc_body, 0)
    g4(1)
    g4(2)
    g2(3)
    g1(4)
    g1z(4)
    spread_wait(1, pr)
    from_hbm["fe"].wait()
    from_hbm["te"].wait()
    total = sum_of(pr)
    em[...] = (total * jax.nn.sigmoid(total)).astype(BF).astype(F32)
    emb = em[...].astype(BF)
    row_f = jnp.dot(emb, fe[...], preferred_element_type=F32)
    row_t = jnp.dot(emb, te[...], preferred_element_type=F32)
    both = jnp.concatenate([row_f, row_t], axis=1)
    for s in range(16):
        rb[s] = both[s : s + 1, :]
    rr[me] = rb[me]
    spread(2, lambda to: rb.at[to], rr)
    g5(1)
    g5(2)
    unpacked(0, w1)

    conv(xa, w1, put_p, 0, 2)
    conv(xa, w1, put_p, 2, 4)
    g3(3)
    spread_wait(2, rr)
    row = sum_of(rr)
    frozen_row, train_row = row[:, 0:C], row[:, C : 2 * C]

    def p_at(i):
        return p[rows(i, TILE), :]

    def train_at(i):
        return p_at(i) + train_row

    def frozen_at(i):
        return p_at(i) + frozen_row

    mean, inverse = stats(train_at, g_ref)
    g4(3)

    def y_body(i, c):
        v = (train_at(i) - mean) * inverse
        y1[rows(i, TILE), :] = v
        put_shifted(v * jax.nn.sigmoid(v), xb, i, 1)
        return c

    lax.fori_loop(0, STEPS, y_body, 0)
    g2(4)
    g1(5)
    g1z(5)
    g5(3)
    unpacked(1, w2)
    conv_back(d3, w2, put_p, 0, 2)
    conv_back(d3, w2, put_p, 2, 4)
    g3(4)
    zero = jnp.zeros((8, C), F32)

    def dy_body(i, s):
        v = y1[rows(i, TILE), :]
        sig = jax.nn.sigmoid(v)
        dy = p_at(i) * sig * (1.0 + v * (1.0 - sig))
        p[rows(i, TILE), :] = dy
        return s[0] + fold(dy), s[1] + fold(dy * v)

    s1, s2 = lax.fori_loop(0, STEPS, dy_body, (zero, zero))
    m1, m2 = group_mean(s1, g_ref), group_mean(s2, g_ref)

    def dp_body(i, s):
        d = (p_at(i) - m1 - y1[rows(i, TILE), :] * m2) * inverse
        dq[rows(i, TILE, COLS), :] = d.astype(BF)
        return s + fold(d)

    es[me] = jnp.sum(lax.fori_loop(0, STEPS, dp_body, zero), axis=0, keepdims=True)
    spread(3, lambda to: es.at[me], es)
    grad_dots(xa, dq, 0)
    g2(5)
    grad_dots(xa, dq, 1)
    grad_dots(xa, dq, 2)
    g4(4)
    packed(out_b)
    step(0, 1)
    step(1, 1)

    grad_dots(xb, dp, 0)
    g3(5)
    grad_dots(xb, dp, 1)
    step(0, 2)
    step(1, 2)
    grad_dots(xb, dp, 2)
    packed(out_a)
    step(2, 1)

    def write_control(m, acc):
        mixed = lat[rows(m, MT), :].astype(F32) + hint[rows(m, MT), :].astype(F32)
        ctl[rows(m, MT), :] = (mixed + acc).astype(BF)

    conv(xb, w2, write_control, 0, 2)
    g4(5)
    step(0, 3)
    conv(xb, w2, write_control, 2, 3)
    step(1, 3)
    conv(xb, w2, write_control, 3, 4)
    step(2, 2)
    dz = lax.dot_general(ctl[...], sg[...], (((0,), (0,)), ((), ())), preferred_element_type=F32)
    for d in range(16):
        for h in range(2):
            at = d * 20 + h * 10
            out_a[d % 2, d // 2, AT : AT + 10, h * C : (h + 1) * C] = dz[at : at + 10, :].astype(BF)
    step(3, 1)
    g5(4)
    unpacked(2, v1)
    step(0, 4)

    conv(xf, v1, put_p, 0, 1)
    spread_wait(3, es)
    de = lax.dot_general(
        em[...], stacked(es), (((0,), (0,)), ((), ())), preferred_element_type=F32, precision=EXACT
    )
    for h in range(2):
        cur_b[0, AT : AT + 40, h * C : (h + 1) * C] = de[h * 40 : (h + 1) * 40, :].astype(BF)
    step(3, 2)
    step(1, 4)
    conv(xf, v1, put_p, 1, 2)
    step(2, 3)
    conv(xf, v1, put_p, 2, 3)
    step(0, 5)
    conv(xf, v1, put_p, 3, 4)
    step(3, 3)
    step(1, 5)
    mean_f, inverse_f = stats(frozen_at, g_ref)
    step(0, 6)
    step(2, 4)

    def frozen_body(i, c):
        v = (frozen_at(i) - mean_f) * inverse_f
        put_shifted(v * jax.nn.sigmoid(v), xf, i, 1)
        return c

    lax.fori_loop(0, STEPS, frozen_body, 0)
    g5(5)
    unpacked(3, v2)
    step(1, 6)

    def write_skip(m, acc):
        out = lat[rows(m, MT), :].astype(F32) + acc
        out = out + jnp.dot(ctl[rows(m, MT), :], wz[...], preferred_element_type=F32)
        skip[:, pl.ds(pl.multiple_of(m * MT, MT), MT)] = out.T.astype(BF)

    conv(xf, v2, write_skip, 0, 1)
    step(0, 7)
    step(2, 5)
    conv(xf, v2, write_skip, 1, 2)
    step(3, 4)
    step(1, 7)
    conv(xf, v2, write_skip, 2, 3)
    step(2, 6)
    conv(xf, v2, write_skip, 3, 4)
    skip_out = pltpu.make_async_copy(skip, skip_h, o_sem.at[0])
    skip_out.start()
    step(3, 5)
    step(2, 7)
    step(3, 6)
    step(3, 7)
    for n in range(4):
        step(n, 8)
    tot_a = cur_a[2].astype(F32) + got_a[2].astype(F32)
    tot_b = cur_b[2].astype(F32) + got_b[2].astype(F32)
    row_at = lax.broadcasted_iota(jnp.int32, (AT + 40, 2 * C), 0)
    own_a = jnp.where((row_at < HALF) | ((row_at >= AT) & (row_at < AT + 10)), jnp.pad(tot_a, ((0, 24), (0, 0))), 0.0)
    own_b = jnp.where((row_at < HALF) | (row_at >= AT), tot_b, 0.0)
    sq = jnp.sum(own_a * own_a, axis=0, keepdims=True) + jnp.sum(own_b * own_b, axis=0, keepdims=True)
    nr[me] = jnp.broadcast_to(jnp.sum(sq, axis=1, keepdims=True), (1, 128))
    spread(4, lambda to: nr.at[me], nr)
    for u in range(6):
        g_sent(u)
    for n in range(4):
        step_sent(n)
    spread_sent(0, wv)
    spread_sent(1, pr)
    spread_sent(2, rr)
    spread_sent(3, es)
    skip_out.wait()
    spread_wait(4, nr)
    norm = jnp.sqrt(sum_of(nr)[:, 0:1] + 1e-06)
    scale = jnp.minimum(1.0, clip_limit / norm)
    onorm[...] = jnp.broadcast_to(norm, (8, 128))
    oa[...] = tot_a * scale
    ob[...] = tot_b * scale
    results = []
    for n, (src, dst) in enumerate(((oa, oa_h), (ob, ob_h), (onorm, onorm_h))):
        results.append(pltpu.make_async_copy(src, dst, o_sem.at[n + 1]))
        results[-1].start()
    for c in results:
        c.wait()
    spread_sent(4, nr)


def vm(shape, dtype=BF):
    return pltpu.VMEM(shape, dtype)


SCRATCH = [
    vm((C, POS)), vm((C, POS)), vm((C, POS)), vm((1, C), F32), vm((180, C)), vm((180, C)), vm((20, TEMB)),
    vm((80, C)), vm((180, C)), vm((180, C)), vm((80, C)), vm((20, C)),
    vm((C, POS)), vm((AT + 16, 2 * C), F32), vm((AT + 40, 2 * C), F32), vm((8, 128), F32),
    pltpu.SemaphoreType.DMA((12,)), pltpu.SemaphoreType.DMA((4,)),
    vm((POS, C)), vm((POS, C)), vm((POS, C)), vm((C, C)),
    vm((POS + 2 * COLS, 3 * C)), vm((POS + 2 * COLS, 3 * C)), vm((POS + 2 * COLS, 3 * C)),
    vm((POS + 2 * COLS, 3 * C)), vm((POS + 2 * COLS, C)), vm((POS + 2 * COLS, C)),
    vm((POS, C), F32), vm((POS, C), F32), vm((POS, C)), vm((9 * C, C)),
    vm((9 * C, C)), vm((9 * C, C)), vm((9 * C, C)), vm((9 * C, C)), vm((C, C)),
    vm((2, 8, HALF, 2 * C)), vm((2, 8, HALF, 2 * C)), vm((2, 8, HALF, 2 * C)), vm((2, 8, HALF, 2 * C)),
    vm((2, 8, 10, 2 * C)),
    vm((16, 1, C), F32), vm((16, 16, 80), F32), vm((16, 16, 80), F32), vm((16, 1, 2 * C), F32),
    vm((16, 1, 2 * C), F32), vm((16, 80), F32), vm((16, 1, C), F32),
    vm((16, 1, 128), F32),
    vm((2, 8, AT + 16, 2 * C)), vm((2, 8, AT, 2 * C)),
    vm((8, AT + 16, 2 * C)), vm((8, AT, 2 * C)),
    vm((2, AT + 16, 2 * C)), vm((2, AT, 2 * C)),
    vm((2, 2, AT + 16, 2 * C)), vm((2, 2, AT, 2 * C)),
    vm((AT + 16, 2 * C)), vm((AT, 2 * C)),
    vm((3, AT + 16, 2 * C)), vm((3, AT + 40, 2 * C)),
    vm((3, AT + 16, 2 * C)), vm((3, AT + 40, 2 * C)),
    pltpu.SemaphoreType.DMA((6, 2)), pltpu.SemaphoreType.DMA((6, 9)),
    pltpu.SemaphoreType.DMA((5,)), pltpu.SemaphoreType.DMA((5,)),
    pltpu.SemaphoreType.DMA((4, 3)), pltpu.SemaphoreType.DMA((4, 9)),
]


def finish(skip_in, a_in, b_in, n_in, skip_out, o1_h, o2_h, oe_h, oz_h, on_h, sk, a, b, nv, o1, o2, oe, oz, on, i_sem, o_sem):
    loads = [
        pltpu.make_async_copy(src, dst, i_sem.at[n])
        for n, (src, dst) in enumerate(((skip_in, sk), (a_in, a), (b_in, b), (n_in, nv)))
    ]
    for c in loads:
        c.start()
    stores = []

    def put(src, dst):
        stores.append(pltpu.make_async_copy(src, dst, o_sem.at[len(stores)]))
        stores[-1].start()

    loads[0].wait()
    put(sk, skip_out)
    for c in loads[1:]:
        c.wait()
    for h in range(2):
        c = slice(h * C, (h + 1) * C)
        o2[h * HALF : (h + 1) * HALF, :] = a[0:HALF, c]
        oz[h * 10 : (h + 1) * 10, :] = a[AT : AT + 10, c]
        o1[h * HALF : (h + 1) * HALF, :] = b[0:HALF, c]
        oe[h * 40 : (h + 1) * 40, :] = b[AT : AT + 40, c]
    on[...] = nv[0:1, 0:1]
    for src, dst in ((o1, o1_h), (o2, o2_h), (oe, oe_h), (oz, oz_h), (on, on_h)):
        put(src, dst)
    for c in stores:
        c.wait()


def wave_of(timestep):
    half = C // 2
    freqs = jnp.exp(-math.log(10000.0) * jnp.arange(half).astype(F32) / half)
    angles = timestep.astype(F32)[:, None] * freqs[None, :]
    return jnp.concatenate([jnp.cos(angles), jnp.sin(angles)], axis=1).astype(BF).astype(F32)


def shards(
    latent, hint, timestep, skip_grad, frozen_one, frozen_two, time_weight, frozen_emb,
    train_one, train_two, train_emb, zero_weight,
):
    spec = pl.BlockSpec(memory_space=pl.ANY)
    held = pl.pallas_call(
        kernel,
        out_shape=(
            jax.ShapeDtypeStruct((C, POS), BF),
            jax.ShapeDtypeStruct((AT + 16, 2 * C), F32),
            jax.ShapeDtypeStruct((AT + 40, 2 * C), F32),
            jax.ShapeDtypeStruct((8, 128), F32),
        ),
        in_specs=[spec] * 12,
        out_specs=[spec] * 4,
        scratch_shapes=SCRATCH,
        compiler_params=pltpu.CompilerParams(
            vmem_limit_bytes=67043328, collective_id=0, has_side_effects=True
        ),
    )(
        latent[0].T, hint[0].T, skip_grad[0].T, wave_of(timestep), frozen_one, frozen_two, time_weight, frozen_emb,
        train_one, train_two, train_emb, zero_weight,
    )
    skip, g1, g2, ge, gz, norm = pl.pallas_call(
        finish,
        out_shape=(
            jax.ShapeDtypeStruct((C, POS), BF),
            jax.ShapeDtypeStruct((180, C), F32),
            jax.ShapeDtypeStruct((180, C), F32),
            jax.ShapeDtypeStruct((80, C), F32),
            jax.ShapeDtypeStruct((20, C), F32),
            jax.ShapeDtypeStruct((1, 1), F32),
        ),
        in_specs=[pl.BlockSpec(memory_space=pltpu.HBM)] * 4,
        out_specs=[spec] * 6,
        scratch_shapes=[
            vm((C, POS)), vm((AT + 16, 2 * C), F32), vm((AT + 40, 2 * C), F32), vm((8, 128), F32),
            vm((180, C), F32), vm((180, C), F32), vm((80, C), F32), vm((20, C), F32), vm((1, 1), F32),
            pltpu.SemaphoreType.DMA((4,)), pltpu.SemaphoreType.DMA((6,)),
        ],
        compiler_params=pltpu.CompilerParams(vmem_limit_bytes=67043328),
    )(*held)
    return (skip.T[None], g1, g2, ge, gz, norm[0, 0])


def solution(mesh):
    data, rows_of = P(("dp", "fsdp"), None, None), P("fsdp", None)
    return jax.shard_map(
        shards,
        mesh=mesh,
        in_specs=(data, data, P(("dp", "fsdp")), data) + (rows_of,) * 8,
        out_specs=(data, rows_of, rows_of, rows_of, rows_of, P()),
        check_vma=False,
    )
```

time: 127 us -> 107 us (0.84)
  Pallas kernels: 117 us -> 104 us
  local copies, waits for them, and re-layouts: 5.46 us -> 0.01 us
  between operations: 3.09 us -> 1.51 us
    pallas_call x1, Pallas kernels: 117 us -> 102 us  [shards(): pl.pallas_call(kernel, out_shape=(jax.ShapeDtypeStruct((C, POS), BF), jax...]
    unnamed x13 -> x0, local copies, waits for them, and re-layouts: 5.45 us -> none
    pallas_call x0 -> x1, Pallas kernels: none -> 2.35 us  [shards(): pl.pallas_call(finish, out_shape=(jax.ShapeDtypeStruct((C, POS), BF), jax...]
where the time goes in v2:
time: 107 us; the launch traced here: 106 us
  Pallas kernels  104 us (97%)
  between operations  1.51 us (1%)
    pallas_call x1, Pallas kernels, shards(): pl.pallas_call(kernel, out_shape=(jax.ShapeDtypeStruct((C, POS), BF), jax...  102 us
    pallas_call x1, Pallas kernels, shards(): pl.pallas_call(finish, out_shape=(jax.ShapeDtypeStruct((C, POS), BF), jax...  2.35 us

profile of v2, /device:TPU:1, one launch (start us, length us, event | category | flops | bytes accessed | tf_op | source)
XLA Modules:
  0.0 106.4 jit_solution(11330544721316154177)
XLA Ops:
  1.4 0.6 maximum_convert_fusion.wave_h
  2.0 101.8 %shard_map.163 = (bf16[320,1024]{1,0:T(8,128)(2,1)}, f32[112,640]{1,0:T(8,128)}, f32[136,640]{1,0:T(8,128)}, f32[8,128]{1,0:T(8,128)}) custom-call(bf16[320,1024]{1,0:T(8,128)(2,1)} %bitcast.14, bf16[320,1024]{1,0:T(8,128)(2,1)} %bitcast.15, bf16[320,1024]{1,0:T(8,128)(2,1)} %bitcast.16, f32[1,320]{1,0:T(1,128)} %maximum_convert_fusion.wave_h, ...), custom_call_target="tpu_custom_call" | custom-call | tf_op jit(solution)/shard_map/pallas_call | solution.py:720
  103.8 2.3 %shard_map.164 = (bf16[320,1024]{1,0:T(8,128)(2,1)}, f32[180,320]{1,0:T(8,128)}, f32[180,320]{1,0:T(8,128)}, f32[80,320]{1,0:T(8,128)}, f32[20,320]{1,0:T(8,128)}, /*index=5*/f32[1,1]{1,0:T(1,128)}) custom-call(bf16[320,1024]{1,0:T(8,128)(2,1)} %get-tuple-element.16.skip_in, f32[112,640]{1,0:T(8,128)} %get-tuple-element.17.a_in, ...), custom_call_target="tpu_custom_call" | custom-call | tf_op jit(solution)/shard_map/pallas_call | solution.py:738
  (3 shorter events, 0.1 us)
